TPU v7x, 32 devices: a whole 2x2x4 slice. The times are simulated.
32 devices in a mesh: seq: 8 (over z, core), vocab: 4 (over y, x).
Axes of the slice: x: 2, y: 2, z: 4, core: 2. Of those that a mesh axis runs over, the one named last changes fastest.
Arguments:
- token_ids: int32 [1024], P('seq'), may hold values from 0 to 76031, as said below
- routes: int32 [256, 1], P('seq'), may hold values from 0 to 7; in each aligned block of 32 rows (0 to 31, 32 to 63, ...) at most 8 rows name the same one
- splice_start: int32 [8], P('seq'), may hold values from 0 to 64
- vision: bfloat16 [256, 5120], P('seq'), may hold values from -6 to 6
- ln_gain: float32 [1280], replicated, may hold values from 0.25 to 1.75
- table: bfloat16 [76032, 8192], P('seq', 'vocab'), may hold values from -6 to 6
- w_fc1: bfloat16 [5120, 5120], P('seq', 'vocab'), may hold values from -0.078125 to 0.078125
- w_fc2: bfloat16 [5120, 8192], P('seq', 'vocab'), may hold values from -0.078125 to 0.078125
Outputs:
- embedded: bfloat16 [1024, 8192], P('seq', 'vocab')
Inputs may be any that keep to these rules, and one draw needn't show every extreme that they name: `routes`: among the rows of one shard of 32 rows no sequence is named by more than 8 rows. `token_ids`: split the vocabulary into 8 equal ranges of consecutive ids; within one sequence of 128 tokens at most 32 ids fall in one range, and every sequence has a range with exactly 32.
All inputs are finite; a program needn't handle non-finite values.
Results may differ from a plain program's by a relative error of at most 0.0055.
Values may be sent and summed in bfloat16 or wider, within the bound.
A program may use at most 128 MiB of HBM per device.

v0:
```python
import math

import jax
import jax.numpy as jnp
from jax import lax
from jax.sharding import PartitionSpec as P


def layer_norm(vision, ln_gain):
    rows = vision.shape[0]
    values = vision.astype(jnp.float32).reshape(rows, 4, ln_gain.shape[0])
    center = values - jnp.mean(values, axis=-1, keepdims=True)
    spread = jnp.mean(center * center, axis=-1, keepdims=True)
    normed = center / jnp.sqrt(spread + 1e-06) * ln_gain
    return normed.reshape(rows, 4 * ln_gain.shape[0]).astype(jnp.bfloat16)


def on_device(token_ids, routes, splice_start, vision, ln_gain, table, w_fc1, w_fc2):
    seq_count = lax.axis_size("seq")
    seq_index = lax.axis_index("seq")
    all_ids, all_routes = (
        lax.all_gather(token_ids, "seq", axis=0, tiled=True),
        lax.all_gather(routes[:, 0], "seq", axis=0, tiled=True),
    )
    shard_rows = table.shape[0]
    local_rows = token_ids.shape[0]
    columns = jnp.arange(shard_rows, dtype=jnp.int32) + seq_index * shard_rows
    block_rows = math.gcd(lax.axis_size("seq") * local_rows, 512)
    chosen = all_ids.reshape(lax.axis_size("seq") * local_rows // block_rows, block_rows)

    def one_block(block_ids):
        picker = (block_ids[:, None] == columns[None, :]).astype(jnp.bfloat16)
        return jnp.dot(picker, table, preferred_element_type=jnp.float32)

    text = lax.psum_scatter(
        lax.map(one_block, chosen)
        .reshape(lax.axis_size("seq") * local_rows, table.shape[1])
        .astype(jnp.bfloat16),
        "seq",
        scatter_dimension=0,
        tiled=True,
    ).astype(jnp.float32)
    normed = layer_norm(vision, ln_gain)
    slot_rows = vision.shape[0]
    input_cols = lax.all_to_all(normed, "seq", split_axis=1, concat_axis=0, tiled=True)
    part = input_cols
    pre = lax.psum_scatter(
        jnp.dot(part, w_fc1, preferred_element_type=jnp.float32),
        "seq",
        scatter_dimension=0,
        tiled=True,
    )
    hidden = jax.nn.gelu(pre, approximate=False).astype(jnp.bfloat16)
    hidden_full = lax.all_gather(hidden, "vocab", axis=1, tiled=True)
    hidden_cols = lax.all_to_all(hidden_full, "seq", split_axis=1, concat_axis=0, tiled=True)
    part = hidden_cols
    merged_sum = lax.psum_scatter(
        jnp.dot(part, w_fc2, preferred_element_type=jnp.float32).astype(jnp.bfloat16),
        "seq",
        scatter_dimension=0,
        tiled=True,
    )
    own_routes = routes[:, 0]
    pair_cap = 2 * slot_rows // seq_count
    owner_hot = (own_routes[:, None] == jnp.arange(seq_count, dtype=jnp.int32)[None, :]).astype(
        jnp.int32
    )
    earlier = jnp.cumsum(owner_hot, axis=0) - owner_hot
    rank = jnp.sum(earlier * owner_hot, axis=1)
    slot_of = own_routes * pair_cap + rank
    selector = (
        slot_of[None, :] == jnp.arange(seq_count * pair_cap, dtype=jnp.int32)[:, None]
    ).astype(jnp.bfloat16)
    outgoing = jnp.dot(selector, merged_sum, preferred_element_type=jnp.float32).astype(
        jnp.bfloat16
    )
    arrived = lax.all_to_all(outgoing, "seq", split_axis=0, concat_axis=0, tiled=True)
    sender_counts = jnp.sum(
        (all_routes.reshape(seq_count, slot_rows) == seq_index).astype(jnp.int32), axis=1
    )
    sender_offset = jnp.cumsum(sender_counts) - sender_counts
    within = jnp.arange(pair_cap, dtype=jnp.int32)
    position = (splice_start[0] + sender_offset[:, None] + within[None, :]).reshape(-1)
    live = (within[None, :] < sender_counts[:, None]).reshape(-1)
    placer = (
        (position[None, :] == jnp.arange(local_rows, dtype=jnp.int32)[:, None]) & live[None, :]
    ).astype(jnp.bfloat16)
    image_part = jnp.dot(placer, arrived, preferred_element_type=jnp.float32)
    is_image = jnp.sum(placer.astype(jnp.float32), axis=1) > 0.5
    return jnp.where(is_image[:, None], image_part, text).astype(jnp.bfloat16)


def solution(mesh):
    in_specs = (
        P("seq"),
        P("seq", None),
        P("seq"),
        P("seq", None),
        P(),
        P("seq", "vocab"),
        P("seq", "vocab"),
        P("seq", "vocab"),
    )
    out_specs = P("seq", "vocab")
    return jax.shard_map(
        on_device, mesh=mesh, in_specs=in_specs, out_specs=out_specs, check_vma=False
    )
```

profile of v0, /device:TPU:0, one launch (start us, length us, event | category | flops | bytes accessed | tf_op | source)
XLA Modules:
  0.0 211.0 jit_solution(2513353129289879950)
XLA Ops:
  6.5 0.0 copy-start
  6.5 0.0 copy-start.1
  6.5 0.0 reduce-scatter.4.cloned.1.call-start
  6.5 1.4 reshape.111
  8.0 0.2 reduce_sum.48
  8.2 0.3 multiply_reduce_fusion
  8.5 0.2 div.19
  8.7 0.1 copy.19
  8.8 0.1 sub.25
  8.9 1.0 copy.18
  9.9 0.0 copy-done.1
  9.9 1.3 multiply_convert_fusion
  11.2 0.0 copy-start.3
  11.3 17.3 %all_to_all.50 = bf16[32,8,640]{2,0,1:T(8,128)(2,1)S(1)} all-to-all(bf16[32,8,640]{2,0,1:T(8,128)(2,1)S(1)} %bitcast.57), channel_id=1, replica_groups=mesh['seq'=8,'vocab'=4] {'seq'}, dimensions={1} | all-to-all | bytes 655360 | tf_op jit(solution)/shard_map/all_to_all | solution.py:45
  28.5 3.2 %fusion.29 = f32[256,1280]{1,0:T(8,128)} fusion(bf16[256,640]{1,0:T(8,128)(2,1)S(1)} %bitcast.56, bf16[640,1280]{1,0:T(8,128)(2,1)} %param.16), kind=kOutput, calls=%fused_computation.58 | convolution fusion | flops 419430400 | bytes 3276800 | tf_op jit(solution)/shard_map/dot_general | solution.py:48
  31.7 0.0 reduce-scatter.4.cloned.1.call-update
  31.7 32.3 %reduce-scatter.4.cloned.1.call-done = f32[32,1280]{1,0:T(8,128)} async-done(((f32[256,1280]{1,0:T(8,128)}), f32[32,1280]{1,0:T(8,128)}) %reduce-scatter.4.cloned.1.call-update) | async-done | bytes 163856 | tf_op jit(solution)/shard_map/reduce_scatter | solution.py:47
  64.1 1.3 fusion.13
  65.3 9.6 %all_gather.10 = bf16[32,5120]{1,0:T(8,128)(2,1)S(1)} all-gather(bf16[32,1280]{1,0:T(8,128)(2,1)S(1)} %fusion.13), channel_id=1, replica_groups=mesh['seq'=8,'vocab'=4] {'vocab'}, dimensions={1}, use_global_device_ids=true | all-gather | bytes 409600 | tf_op jit(solution)/shard_map/all_gather | solution.py:54
  74.9 0.8 copy.22
  75.7 3.4 %all-to-all-start.1 = ((bf16[32,8,640]{2,0,1:T(8,128)(2,1)}), bf16[32,8,640]{2,0,1:T(8,128)(2,1)S(1)}, u32[]{:S(2)}, u32[]{:S(2)}) async-start(bf16[32,8,640]{2,0,1:T(8,128)(2,1)} %bitcast.42), calls=%async_computation.2 | async-start | bytes 655360 | tf_op jit(solution)/shard_map/all_to_all | solution.py:55
  79.1 0.0 reduce-scatter.6.cloned.1.call-start
  79.2 0.0 copy-done.3
  79.2 13.0 %all-gather.1 = s32[8,1,128]{2,1,0:T(1,128)S(1)} all-gather(s32[1,1,128]{2,1,0:T(1,128)S(1)} %bitcast.65), channel_id=1, replica_groups=mesh['seq'=8,'vocab'=4] {'seq'}, dimensions={0}, use_global_device_ids=true | all-gather | bytes 4608 | tf_op jit(solution)/shard_map/all_gather | solution.py:22
  92.2 0.5 broadcast.72
  92.7 0.6 reduce.3
  93.3 0.0 all-to-all-done.1
  93.3 0.0 copy-done
  93.4 2.0 convolution_convert_fusion
  95.3 0.0 reduce-scatter.6.cloned.1.call-update
  95.3 0.0 reduce-scatter.8.cloned.1.call-start
  95.4 53.3 %while.11 = (s32[]{:T(128)}, bf16[2,512,2048]{2,1,0:T(8,128)(2,1)}, s32[2,512]{1,0:T(2,128)S(1)}, bf16[9504,2048]{1,0:T(8,128)(2,1)}, s32[]{:T(128)}, /*index=5*/s32[]{:T(128)}) while((s32[]{:T(128)}, bf16[2,512,2048]{2,1,0:T(8,128)(2,1)}, s32[2,512]{1,0:T(2,128)S(1)}, bf16[9504,2048]{1,0:T(8,128)(2,1)}, s32[]{:T(128)}, ...), condition=%wide.region_10.11_spmd.clone, body=%wide.region_9.10_spmd.clone.sunk | while | flops 19936208896 | bytes 43204952 | solution.py:36
  95.4 26.6 %bitcast_dynamic-update-slice_fusion.3 = bf16[2,512,2048]{2,1,0:T(8,128)(2,1)} fusion(bf16[2,512,2048]{2,1,0:T(8,128)(2,1)} %get-tuple-element.96, s32[]{:T(128)S(6)} %copy.27, bf16[9504,2048]{1,0:T(8,128)(2,1)} %get-tuple-element.104, s32[9504]{0:T(1024)S(1)} %iota_add_fusion.3, s32[512]{0:T(512)S(1)} %bitcast.61), kind=kOutput, calls=%fused_computation.5.clone.1 | convolution fusion | flops 19936198656 | bytes 43162756 | tf_op jit(solution)/shard_map/while/body/eval_jaxpr/dot_general | solution.py:33
  122.1 26.6 %bitcast_dynamic-update-slice_fusion.3 = bf16[2,512,2048]{2,1,0:T(8,128)(2,1)} fusion(bf16[2,512,2048]{2,1,0:T(8,128)(2,1)} %get-tuple-element.96, s32[]{:T(128)S(6)} %copy.27, bf16[9504,2048]{1,0:T(8,128)(2,1)} %get-tuple-element.104, s32[9504]{0:T(1024)S(1)} %iota_add_fusion.3, s32[512]{0:T(512)S(1)} %bitcast.61), kind=kOutput, calls=%fused_computation.5.clone.1 | convolution fusion | flops 19936198656 | bytes 43162756 | tf_op jit(solution)/shard_map/while/body/eval_jaxpr/dot_general | solution.py:33
  148.7 0.0 copy-start.2
  148.7 0.0 copy-start.4
  148.7 0.0 reduce-scatter.8.cloned.1.call-update
  148.7 0.6 copy-done.2
  149.3 0.1 fusion.25
  149.4 0.1 reduce_window_sum.18
  149.5 0.0 copy-done.4
  149.5 0.6 dynamic-slice
  150.7 0.2 select_reduce_fusion
  150.9 0.1 multiply_add_fusion
  151.0 8.5 %all-reduce = s32[256]{0:T(256)S(1)} all-reduce(s32[256]{0:T(256)S(1)} %get-tuple-element.57), channel_id=2, replica_groups=mesh['seq'=8,'vocab'=4] {'seq'}, use_global_device_ids=true, to_apply=%add | all-reduce | flops 256 | bytes 2048
  159.6 0.1 reshape.113
  159.6 0.1 reduce_sum.45
  159.8 0.2 reduce-window.8
  160.6 0.1 iota_add_fusion.1
  160.7 0.1 add.71
  160.8 0.0 reduce-scatter.6.cloned.1.call-done
  160.8 1.8 fusion.9
  162.6 3.4 %all-to-all-start.2 = ((bf16[8,8,2048]{2,1,0:T(8,128)(2,1)}), bf16[8,8,2048]{2,1,0:T(8,128)(2,1)S(1)}, u32[]{:S(2)}, u32[]{:S(2)}) async-start(bf16[8,8,2048]{2,1,0:T(8,128)(2,1)} %fusion.9), calls=%async_computation.4 | async-start | bytes 524288 | tf_op jit(solution)/shard_map/all_to_all | solution.py:77
  166.0 0.1 iota_compare_fusion.4
  166.1 0.1 lt.23
  166.2 0.1 convert_reduce_fusion
  166.3 13.9 %all-to-all-done.2 = bf16[8,8,2048]{2,1,0:T(8,128)(2,1)S(1)} async-done(((bf16[8,8,2048]{2,1,0:T(8,128)(2,1)}), bf16[8,8,2048]{2,1,0:T(8,128)(2,1)S(1)}, u32[]{:S(2)}, u32[]{:S(2)}) %all-to-all-start.2) | async-done | bytes 262176 | tf_op jit(solution)/shard_map/all_to_all | solution.py:77
  180.2 22.0 %reduce-scatter.8.cloned.1.call-done = bf16[128,2048]{1,0:T(8,128)(2,1)} async-done(((bf16[1024,2048]{1,0:T(8,128)(2,1)}), bf16[128,2048]{1,0:T(8,128)(2,1)}) %reduce-scatter.8.cloned.1.call-update) | async-done | bytes 524304 | tf_op jit(solution)/shard_map/reduce_scatter | solution.py:35
  202.2 2.3 %fusion.8 = bf16[128,2048]{1,0:T(8,128)(2,1)} fusion(bf16[128,2048]{1,0:T(8,128)(2,1)} %reduce-scatter.8.cloned.1.call-done, pred[128]{0:T(512)(128)(4,1)S(1)} %broadcast_compare_fusion, bf16[8,8,2048]{2,1,0:T(8,128)(2,1)S(1)} %all-to-all-done.2, s32[64]{0:T(128)S(1)} %add.71, pred[64]{0:T(512)(128)(4,1)S(1)} %lt.23), kind=kOutput, calls=%fused_computation.10 | convolution fusion | flops 34357248 | bytes 1311168 | tf_op jit(solution)/shard_map/dot_general | solution.py:88
  (15 shorter events, 0.1 us)
Async XLA Ops:
  6.5 86.8 %copy-start = (bf16[640,2048]{1,0:T(8,128)(2,1)S(1)}, bf16[640,2048]{1,0:T(8,128)(2,1)}, u32[]{:S(2)}) copy-start(bf16[640,2048]{1,0:T(8,128)(2,1)} %param.17) | copy-start | bytes 7864324
  6.5 3.4 %copy-start.1 = (f32[1280]{0:T(1024)S(1)}, f32[1280]{0:T(1024)}, u32[]{:S(2)}) copy-start(f32[1280]{0:T(1024)} %param.14) | copy-start | bytes 15364
  6.5 57.5 %reduce-scatter.4.cloned.1.call-start = ((), (), s32[]{:S(2)}) async-start(), calls=%async_computation.6 | async-start | bytes 1474560 | tf_op jit(solution)/shard_map/reduce_scatter | solution.py:47
  11.2 68.0 %copy-start.3 = (s32[128]{0:T(128)S(1)}, s32[128]{0:T(128)}, u32[]{:S(2)}) copy-start(s32[128]{0:T(128)} %param.10) | copy-start | bytes 1540
  75.7 17.6 %all-to-all-start.1 = ((bf16[32,8,640]{2,0,1:T(8,128)(2,1)}), bf16[32,8,640]{2,0,1:T(8,128)(2,1)S(1)}, u32[]{:S(2)}, u32[]{:S(2)}) async-start(bf16[32,8,640]{2,0,1:T(8,128)(2,1)} %bitcast.42), calls=%async_computation.2 | async-start | bytes 655360 | tf_op jit(solution)/shard_map/all_to_all | solution.py:55
  79.1 81.6 %reduce-scatter.6.cloned.1.call-start = ((), (), s32[]{:S(2)}) async-start(), calls=%async_computation.7 | async-start | bytes 1179648 | tf_op jit(solution)/shard_map/reduce_scatter | solution.py:57
  95.3 106.8 %reduce-scatter.8.cloned.1.call-start = ((), (), s32[]{:S(2)}) async-start(), calls=%async_computation.8 | async-start | bytes 4718592 | tf_op jit(solution)/shard_map/reduce_scatter | solution.py:35
  148.7 0.7 copy-start.2
  148.7 0.8 copy-start.4
  162.6 17.6 %all-to-all-start.2 = ((bf16[8,8,2048]{2,1,0:T(8,128)(2,1)}), bf16[8,8,2048]{2,1,0:T(8,128)(2,1)S(1)}, u32[]{:S(2)}, u32[]{:S(2)}) async-start(bf16[8,8,2048]{2,1,0:T(8,128)(2,1)} %fusion.9), calls=%async_computation.4 | async-start | bytes 524288 | tf_op jit(solution)/shard_map/all_to_all | solution.py:77
Sparse Core Ops, SparseCore 0:
  31.9 32.1 reduce-scatter.3
  95.5 31.7 reduce-scatter.5
  148.8 53.3 reduce-scatter.7
where the time goes:
time: 212 us; the launch traced here: 211 us
  waiting for transfers between devices  68.3 us (32%)
  matrix products  62.4 us (29%)
  blocking collectives  48.4 us (23%)
  between operations  14.6 us (7%)
  starting transfers between devices  6.93 us (3%)
  local copies, waits for them, and re-layouts  5.64 us (3%)
  other arithmetic  4.69 us (2%)
    dot_general x2, matrix products, one_block(): return jnp.dot(picker, table, preferred_element_type=jnp.float32)  53.2 us
    reduce_scatter x1, waiting for transfers between devices, on_device(): lax.psum_scatter(jnp.dot(part, w_fc1, preferred_element_type=jnp.float32)...  32.3 us
    reduce_scatter x1, waiting for transfers between devices, on_device(): lax.psum_scatter(lax.map(one_block, chosen).reshape(lax.axis_size('seq')...  22 us
    all_to_all x1, blocking collectives, on_device(): lax.all_to_all(normed, 'seq', split_axis=1, concat_axis=0, tiled=True)  17.3 us
    all_to_all x1, waiting for transfers between devices, on_device(): lax.all_to_all(outgoing, 'seq', split_axis=0, concat_axis=0, tiled=True)  13.9 us
    all_gather x1, blocking collectives, on_device(): lax.all_gather(token_ids, 'seq', axis=0, tiled=True)  13 us
    all_gather x1, blocking collectives, on_device(): hidden_full = lax.all_gather(hidden, 'vocab', axis=1, tiled=True)  9.59 us
    unnamed x1, blocking collectives  8.54 us
  transfers between devices with their start and end apart: 5, of which 3 were waited for; matrix products, arithmetic and copies ran while one was open for 28% of the time, Pallas kernels for 0%

commit v1 on v0

v1 whole, which is shorter than its diff:
```python
import math

import jax
import jax.numpy as jnp
from jax import lax
from jax.experimental import pallas as pl
from jax.experimental.pallas import tpu as pltpu
from jax.sharding import PartitionSpec as P


TILE = 8


def gather_kernel(ids_ref, pick_ref, table_ref, out_ref, held, sems):
    groups, cap, _ = out_ref.shape

    def issue(g, carry):
        def one(k, c):
            row = pl.multiple_of(ids_ref[g, k] // TILE * TILE, TILE)
            at = pl.multiple_of((g * cap + k) * TILE, TILE)
            pltpu.make_async_copy(
                table_ref.at[pl.ds(row, TILE), :], held.at[pl.ds(at, TILE), :], sems.at[g]
            ).start()
            return c

        return lax.fori_loop(0, cap, one, carry)

    lax.fori_loop(0, groups, issue, 0)

    def finish(g, carry):
        at = pl.multiple_of(g * cap * TILE, TILE)
        block = held.at[pl.ds(at, cap * TILE), :]
        pltpu.make_async_copy(block, block, sems.at[g]).wait()
        out_ref[g] = jnp.dot(
            pick_ref[g], block[...], preferred_element_type=jnp.float32
        ).astype(out_ref.dtype)
        return carry

    lax.fori_loop(0, groups, finish, 0)


def gather_rows(local_ids, table):
    groups, cap = local_ids.shape
    width = table.shape[1]
    lane = jnp.arange(cap * TILE, dtype=jnp.int32)
    slot = jnp.arange(cap, dtype=jnp.int32)[None, :] * TILE + local_ids % TILE
    pick = (slot[:, :, None] == lane[None, None, :]).astype(jnp.bfloat16)
    return pl.pallas_call(
        gather_kernel,
        out_shape=jax.ShapeDtypeStruct((groups, cap, width), table.dtype),
        in_specs=[
            pl.BlockSpec(memory_space=pltpu.SMEM),
            pl.BlockSpec(memory_space=pltpu.VMEM),
            pl.BlockSpec(memory_space=pl.ANY),
        ],
        out_specs=pl.BlockSpec(memory_space=pltpu.VMEM),
        scratch_shapes=[
            pltpu.VMEM((groups * cap * TILE, width), table.dtype),
            pltpu.SemaphoreType.DMA((groups,)),
        ],
        name="gather_rows",
    )(local_ids, pick, table)


def route_plan(token_ids, routes, splice_start, shard_rows):
    seq_count = lax.axis_size("seq")
    seq_index = lax.axis_index("seq")
    local_rows = token_ids.shape[0]
    slot_rows = routes.shape[0]
    pair_cap = 2 * slot_rows // seq_count
    id_cap = 2 * local_rows // seq_count
    both = lax.all_gather(jnp.concatenate([token_ids, routes[:, 0]]), "seq", axis=0)
    all_ids, all_routes = both[:, :local_rows], both[:, local_rows:]
    mine = all_ids // shard_rows == seq_index
    place = jnp.cumsum(mine.astype(jnp.int32), axis=1) - 1
    hit = mine[:, None, :] & (
        place[:, None, :] == jnp.arange(id_cap, dtype=jnp.int32)[None, :, None]
    )
    local_ids = jnp.sum(jnp.where(hit, all_ids[:, None, :] - seq_index * shard_rows, 0), axis=2)
    home = token_ids // shard_rows
    same = (home[None, :] == home[:, None]) & (
        jnp.arange(local_rows)[None, :] < jnp.arange(local_rows)[:, None]
    )
    arrive = home * id_cap + jnp.sum(same.astype(jnp.int32), axis=1)
    own = routes[:, 0]
    earlier = (own[None, :] == own[:, None]) & (
        jnp.arange(slot_rows)[None, :] < jnp.arange(slot_rows)[:, None]
    )
    slot_of = own * pair_cap + jnp.sum(earlier.astype(jnp.int32), axis=1)
    selector = (
        slot_of[None, :] == jnp.arange(seq_count * pair_cap, dtype=jnp.int32)[:, None]
    ).astype(jnp.bfloat16)
    counts = jnp.sum((all_routes == seq_index).astype(jnp.int32), axis=1)
    before = jnp.arange(seq_count)[None, :] < jnp.arange(seq_count)[:, None]
    offset = jnp.sum(jnp.where(before, counts[None, :], 0), axis=1)
    within = jnp.arange(pair_cap, dtype=jnp.int32)
    position = jnp.where(
        within[None, :] < counts[:, None],
        splice_start[0] + offset[:, None] + within[None, :],
        -1,
    ).reshape(-1)
    rows = jnp.arange(local_rows, dtype=jnp.int32)
    image = position[None, :] == rows[:, None]
    first = splice_start[0]
    is_image = (rows >= first) & (rows < first + jnp.sum(counts))
    text = (
        arrive[:, None] == jnp.arange(seq_count * id_cap, dtype=jnp.int32)[None, :]
    ) & ~is_image[:, None]
    return local_ids, selector, image.astype(jnp.bfloat16), text.astype(jnp.bfloat16)


def mega_kernel(
    vision_ref, gain_ref, w1_hbm, w2_hbm, text_ref, selector_ref, image_ref, placed_ref, out_ref,
    w1, w2, x_send, x_recv, half_send, half_recv, half_own, cross_send, cross_recv,
    h_send, h_recv, pair_send, pair_recv, pair_own, part_send, part_recv,
    row_send, row_recv, text_recv, total,
    w_sem, x_sems, half_sems, cross_sems, h_send_sems, h_recv_sems,
    pair_sems, part_sems, row_sems, text_sems,
):
    n, voc = lax.axis_size("seq"), lax.axis_size("vocab")
    s, v = lax.axis_index("seq"), lax.axis_index("vocab")
    chips = n // 2
    z, c = s // 2, s % 2
    split = n // voc
    f32, bf16 = jnp.float32, jnp.bfloat16
    slots = vision_ref.shape[0]

    def at(seq, vocab):
        return dict(device_id=(seq, vocab), device_id_type=pl.DeviceIdType.MESH)

    load1 = pltpu.make_async_copy(w1_hbm, w1, w_sem.at[0])
    load2 = pltpu.make_async_copy(w2_hbm, w2, w_sem.at[1])
    load1.start()
    load2.start()

    feeds = s // split
    barrier = pltpu.get_barrier_semaphore()
    for d in range(1, n):
        pl.semaphore_signal(barrier, inc=1, **at(lax.rem(s + d, n), v))
    for e in range(1, voc):
        for j in range(split):
            pl.semaphore_signal(barrier, inc=1, **at(v * split + j, lax.rem(v + e, voc)))

    @pl.when(feeds != v)
    def _():
        for r in range(n):
            pl.semaphore_signal(barrier, inc=1, **at(r, feeds))

    group = gain_ref.shape[1]
    depth = x_send.shape[2]
    for g in range(vision_ref.shape[1] // group):
        values = vision_ref[:, g * group : (g + 1) * group].astype(f32)
        center = values - jnp.mean(values, axis=-1, keepdims=True)
        spread = jnp.mean(center * center, axis=-1, keepdims=True)
        normed = (center / jnp.sqrt(spread + 1e-06) * gain_ref[...]).astype(bf16)
        for k in range(group // depth):
            x_send[g * (group // depth) + k] = normed[:, k * depth : (k + 1) * depth]

    pl.semaphore_wait(barrier, n - 1 + (voc - 1) * split + jnp.where(feeds != v, n, 0))

    def to_peer(source, target, sems, d, seq):
        copy = pltpu.make_async_remote_copy(
            src_ref=source,
            dst_ref=target,
            send_sem=sems.at[0, d],
            recv_sem=sems.at[1, d],
            **at(seq, v),
        )
        copy.start()
        return copy

    copies = []
    for d in range(1, n):
        peer = lax.rem(s + d, n)
        copies.append(to_peer(x_send.at[peer], x_recv.at[c, z], x_sems, d, peer))
    x_recv[c, z] = x_send[s]

    texts = []

    def send_text(ds):
        for d in ds:
            peer = lax.rem(s + d, n)
            texts.append(to_peer(text_ref.at[peer], text_recv.at[s], text_sems, d, peer))

    send_text(TEXT_A(n))
    text_recv[s] = text_ref[s]
    for copy in copies:
        copy.wait()

    def columns(width):
        return 256 if width % 256 == 0 else width

    def summed(lhs_ref, weight, to_sib, from_sib, own, send, recv, sems_pair, sems_part, ds):
        width = weight.shape[1]
        step = columns(width)
        rows = chips * slots
        for core, keep in ((1 - c, False), (c, True)):
            lhs = lhs_ref[core].reshape(rows, weight.shape[0])
            for k in range(0, width, step):
                part = jnp.dot(lhs, weight[:, k : k + step], preferred_element_type=f32)
                if keep:
                    own[:, k : k + step] = part
                else:
                    to_sib[:, k : k + step] = part.astype(bf16)
            if not keep:
                swap = to_peer(to_sib, from_sib, sems_pair, 0, s + 1 - 2 * c)
        swap.wait()
        sent = []
        for d in range(1, chips):
            other = lax.rem(z + d, chips)
            span = pl.ds(pl.multiple_of(other * slots, slots), slots)
            send[d] = (own[span, :] + from_sib[span, :].astype(f32)).astype(bf16)
            sent.append(to_peer(send.at[d], recv.at[d], sems_part, d, other * 2 + c))
        send_text(ds)
        span = pl.ds(pl.multiple_of(z * slots, slots), slots)
        value = own[span, :] + from_sib[span, :].astype(f32)
        for copy in sent:
            copy.wait()
        for d in range(1, chips):
            value = value + recv[d].astype(f32)
        return value

    load1.wait()
    pre = summed(x_recv, w1, half_send, half_recv, half_own, cross_send, cross_recv,
                 half_sems, cross_sems, TEXT_B(n))
    hidden = (0.5 * pre * (1.0 + lax.erf(pre * math.sqrt(0.5)))).astype(bf16)
    inner = h_send.shape[2]
    for j in range(split):
        h_send[j] = hidden[:, j * inner : (j + 1) * inner]

    def hidden_copy(e, j):
        return pltpu.make_async_remote_copy(
            src_ref=h_send.at[j],
            dst_ref=h_recv.at[c, z],
            send_sem=h_send_sems.at[e, j],
            recv_sem=h_recv_sems.at[s],
            **at(v * split + j, lax.rem(v + e, voc)),
        )

    for j in range(split):
        target = v * split + j

        @pl.when(target != s)
        def _():
            hidden_copy(0, j).start()

        @pl.when(target == s)
        def _():
            h_recv[c, z] = h_send[j]

        for e in range(1, voc):
            hidden_copy(e, j).start()
    send_text(TEXT_C(n))
    load2.wait()
    for r in range(n):
        def arrived():
            pltpu.make_async_remote_copy(
                src_ref=h_send.at[0],
                dst_ref=h_recv.at[r % 2, r // 2],
                send_sem=h_send_sems.at[0, 0],
                recv_sem=h_recv_sems.at[r],
                **at(lax.rem(s + 1, n), v),
            ).wait_recv()

        pl.when(jnp.logical_or(r != s, feeds != v))(arrived)

    merged = summed(h_recv, w2, pair_send, pair_recv, pair_own, part_send, part_recv,
                    pair_sems, part_sems, TEXT_D(n)).astype(bf16)

    width = w2.shape[1]
    cap = row_send.shape[1]
    outgoing = jnp.dot(selector_ref[...], merged, preferred_element_type=f32).astype(bf16)
    for t in range(n):
        row_send[t] = outgoing[t * cap : (t + 1) * cap]
    copies = []
    for d in range(1, n):
        peer = lax.rem(s + d, n)
        copies.append(to_peer(row_send.at[peer], row_recv.at[s], row_sems, d, peer))
    row_recv[s] = row_send[s]
    for copy in texts:
        copy.wait()
    step = columns(width)
    found = text_recv[...].reshape(-1, width)
    for k in range(0, width, step):
        total[:, k : k + step] = jnp.dot(
            placed_ref[...], found[:, k : k + step], preferred_element_type=f32
        )
    for copy in copies:
        copy.wait()
    for k in range(0, width, step):
        value = total[:, k : k + step]
        block = row_recv[:, :, k : k + step].astype(f32).reshape(n * cap, step).astype(bf16)
        value = value + jnp.dot(image_ref[...], block, preferred_element_type=f32)
        out_ref[:, k : k + step] = value.astype(bf16)
    for j in range(split):
        for e in range(voc):
            def left():
                hidden_copy(e, j).wait_send()

            if e == 0:
                pl.when(v * split + j != s)(left)
            else:
                left()


def TEXT_A(n):
    return range(1, 2)


def TEXT_B(n):
    return range(2, n // 2)


def TEXT_C(n):
    return range(n // 2, 3 * n // 4)


def TEXT_D(n):
    return range(3 * n // 4, n)


def mega(vision, gain, w1, w2, text, selector, image_pick, text_pick):
    n, voc = lax.axis_size("seq"), lax.axis_size("vocab")
    slots = vision.shape[0]
    rows = n // 2 * slots
    depth, mid = w1.shape
    inner, width = w2.shape
    cap = selector.shape[0] // n
    bf16, f32 = jnp.bfloat16, jnp.float32
    vmem = pl.BlockSpec(memory_space=pltpu.VMEM)
    hbm = pl.BlockSpec(memory_space=pl.ANY)
    dma = pltpu.SemaphoreType.DMA
    return pl.pallas_call(
        mega_kernel,
        out_shape=jax.ShapeDtypeStruct((image_pick.shape[0], width), bf16),
        in_specs=[vmem, vmem, hbm, hbm, vmem, vmem, vmem, vmem],
        out_specs=vmem,
        scratch_shapes=[
            pltpu.VMEM(w1.shape, bf16),
            pltpu.VMEM(w2.shape, bf16),
            pltpu.VMEM((n, slots, depth), bf16),
            pltpu.VMEM((2, n // 2, slots, depth), bf16),
            pltpu.VMEM((rows, mid), bf16),
            pltpu.VMEM((rows, mid), bf16),
            pltpu.VMEM((rows, mid), f32),
            pltpu.VMEM((n // 2, slots, mid), bf16),
            pltpu.VMEM((n // 2, slots, mid), bf16),
            pltpu.VMEM((n // voc, slots, inner), bf16),
            pltpu.VMEM((2, n // 2, slots, inner), bf16),
            pltpu.VMEM((rows, width), bf16),
            pltpu.VMEM((rows, width), bf16),
            pltpu.VMEM((rows, width), f32),
            pltpu.VMEM((n // 2, slots, width), bf16),
            pltpu.VMEM((n // 2, slots, width), bf16),
            pltpu.VMEM((n, cap, width), bf16),
            pltpu.VMEM((n, cap, width), bf16),
            pltpu.VMEM(text.shape, bf16),
            pltpu.VMEM((image_pick.shape[0], width), f32),
            dma((2,)),
            dma((2, n)),
            dma((2, 1)),
            dma((2, n // 2)),
            dma((voc, n // voc)),
            dma((n,)),
            dma((2, 1)),
            dma((2, n // 2)),
            dma((2, n)),
            dma((2, n)),
        ],
        compiler_params=pltpu.CompilerParams(
            collective_id=0, has_side_effects=True, vmem_limit_bytes=40 * 1024 * 1024
        ),
        name="merger",
    )(vision, gain[None, :], w1, w2, text, selector, image_pick, text_pick)


def on_device(token_ids, routes, splice_start, vision, ln_gain, table, w_fc1, w_fc2):
    local_ids, selector, image_pick, text_pick = route_plan(
        token_ids, routes, splice_start, table.shape[0]
    )
    text = gather_rows(local_ids, table)
    return mega(vision, ln_gain, w_fc1, w_fc2, text, selector, image_pick, text_pick)


def solution(mesh):
    in_specs = (
        P("seq"),
        P("seq", None),
        P("seq"),
        P("seq", None),
        P(),
        P("seq", "vocab"),
        P("seq", "vocab"),
        P("seq", "vocab"),
    )
    out_specs = P("seq", "vocab")
    return jax.shard_map(
        on_device, mesh=mesh, in_specs=in_specs, out_specs=out_specs, check_vma=False
    )
```

time: 212 us -> 121 us (0.57)
  the two profiles are of different devices: /device:TPU:0 before, /device:TPU:31 now
where the time goes in v1:
time: 121 us; the launch traced here: 120 us
  Pallas kernels  102 us (84%)
  other arithmetic  6.13 us (5%)
  local copies, waits for them, and re-layouts  5.56 us (5%)
  blocking collectives  4.43 us (4%)
  between operations  2.08 us (2%)
    pallas_call x1, Pallas kernels, mega(): pl.pallas_call(mega_kernel, out_shape=jax.ShapeDtypeStruct((image_pick.sh...  92.2 us
    pallas_call x1, Pallas kernels, gather_rows(): pl.pallas_call(gather_kernel, out_shape=jax.ShapeDtypeStruct((groups, cap...  9.64 us
    unnamed x13, local copies, waits for them, and re-layouts  4.7 us
    unnamed x1, blocking collectives  4.43 us

profile of v1, /device:TPU:31, one launch (start us, length us, event | category | flops | bytes accessed | tf_op | source)
XLA Modules:
  0.0 120.1 jit_solution(3465705943747054290)
XLA Ops:
  0.7 1.2 %dynamic-slice = u32[1]{0:T(128)} dynamic-slice(u32[32]{0:T(128)} %constant.50, u32[]{:T(128)S(6)} %add.79), dynamic_slice_sizes={1} | dynamic-slice | bytes 12
  2.5 0.9 convert_reduce_fusion.1
  3.5 0.7 multiply_add_fusion.1
  4.1 0.7 and_select_fusion
  4.8 0.2 convert_reduce_fusion
  5.0 0.7 multiply_add_fusion
  5.7 0.7 broadcast_in_dim.25.gain_ref
  6.4 0.8 add_dynamic-update-slice_fusion
  7.1 4.4 %all-reduce = s32[1280]{0:T(1024)S(1)} all-reduce(s32[1280]{0:T(1024)S(1)} %add_dynamic-update-slice_fusion), channel_id=2, replica_groups=mesh['seq'=8,'vocab'=4] {'seq'}, use_global_device_ids=true, to_apply=%add | all-reduce | flops 1280 | bytes 10240
  11.6 0.1 reshape.99
  11.6 0.7 convert_reduce_fusion.2
  13.0 0.1 select_reduce_fusion.1
  13.1 0.1 add_select_fusion.2
  13.2 0.1 select_n.45
  13.3 0.3 reduce_window_sum.11
  13.5 0.2 select_reduce_fusion.ids_ref
  13.8 0.0 copy-start.4
  13.8 0.1 fusion.3.placed_ref
  13.9 0.8 fusion.pick_ref
  14.7 0.0 copy-done.4
  14.7 0.0 copy-start.1
  14.7 0.0 copy-start.3
  14.7 9.6 %gather_rows.1.text_ref = bf16[8,32,2048]{2,1,0:T(8,128)(2,1)} custom-call(s32[8,32]{1,0:T(8,128)} %copy-done.4, bf16[8,32,256]{2,1,0:T(8,128)(2,1)} %fusion.pick_ref, bf16[9504,2048]{1,0:T(8,128)(2,1)} %table_ref.1), custom_call_target="tpu_custom_call" | custom-call | tf_op jit(solution)/shard_map/gather_rows/pallas_call | solution.py:48
  24.3 0.0 copy-done.1
  24.4 0.0 copy-done.3
  24.4 0.0 copy-start
  24.4 1.2 %copy-done = bf16[8,32,2048]{2,1,0:T(8,128)(2,1)S(1)} copy-done((bf16[8,32,2048]{2,1,0:T(8,128)(2,1)S(1)}, bf16[8,32,2048]{2,1,0:T(8,128)(2,1)}, u32[]{:S(2)}) %copy-start) | copy-done | bytes 1048600
  25.6 0.0 copy-start.2
  25.6 1.4 %copy-done.2 = bf16[640,1280]{1,0:T(8,128)(2,1)S(1)} copy-done((bf16[640,1280]{1,0:T(8,128)(2,1)S(1)}, bf16[640,1280]{1,0:T(8,128)(2,1)}, u32[]{:S(2)}) %copy-start.2) | copy-done | bytes 1638424
  27.0 92.2 %merger.1 = bf16[128,2048]{1,0:T(8,128)(2,1)S(1)} custom-call(bf16[32,5120]{1,0:T(8,128)(2,1)S(1)} %copy-done.3, f32[1,1280]{1,0:T(1,128)S(1)} %broadcast_in_dim.25.gain_ref, bf16[640,1280]{1,0:T(8,128)(2,1)S(1)} %copy-done.2, bf16[640,2048]{1,0:T(8,128)(2,1)S(1)} %copy-done.1, bf16[8,32,2048]{2,1,0:T(8,128)(2,1)S(1)} %copy-done, ...), custom_call_target="tpu_custom_call" | custom-call | tf_op jit(solution)/shard_map/merger/pallas_call | solution.py:333
  119.3 0.8 copy.12
  (9 shorter events, 0.1 us)
Async XLA Ops:
  13.8 0.9 copy-start.4
  14.7 9.7 %copy-start.1 = (bf16[640,2048]{1,0:T(8,128)(2,1)S(1)}, bf16[640,2048]{1,0:T(8,128)(2,1)}, u32[]{:S(2)}) copy-start(bf16[640,2048]{1,0:T(8,128)(2,1)} %w2_hbm.1) | copy-start | bytes 7864324
  14.7 9.7 %copy-start.3 = (bf16[32,5120]{1,0:T(8,128)(2,1)S(1)}, bf16[32,5120]{1,0:T(8,128)(2,1)}, u32[]{:S(2)}) copy-start(bf16[32,5120]{1,0:T(8,128)(2,1)} %vision_ref.1) | copy-start | bytes 983044
  24.4 1.2 %copy-start = (bf16[8,32,2048]{2,1,0:T(8,128)(2,1)S(1)}, bf16[8,32,2048]{2,1,0:T(8,128)(2,1)}, u32[]{:S(2)}) copy-start(bf16[8,32,2048]{2,1,0:T(8,128)(2,1)} %gather_rows.1.text_ref) | copy-start | bytes 3145732
  25.6 1.4 %copy-start.2 = (bf16[640,1280]{1,0:T(8,128)(2,1)S(1)}, bf16[640,1280]{1,0:T(8,128)(2,1)}, u32[]{:S(2)}) copy-start(bf16[640,1280]{1,0:T(8,128)(2,1)} %w1_hbm.1) | copy-start | bytes 4915204
